TPU v7x, 32 devices: a whole 2x2x4 slice. The times are simulated.
32 devices in a mesh: section: 2 (over core), shard: 4 (over z), rep: 4 (over y, x).
Axes of the slice: x: 2, y: 2, z: 4, core: 2. Of those that a mesh axis runs over, the one named last changes fastest.
Arguments:
- boundary: bfloat16 [2, 2, 16, 256, 1536], P('section', None, ('shard', 'rep')), may hold values from -6 to 6
- lengths: int32 [2, 16], P(None, ('shard', 'rep')), may hold values from 1 to 256, 2457 in all within a row
- in_proj: bfloat16 [2, 1536, 6400], P('section', 'shard'), may hold values from -0.15625 to 0.15625
- dt_proj: bfloat16 [2, 1536, 48], P('section', 'shard'), may hold values from -0.15625 to 0.15625
- out_proj: bfloat16 [2, 3072, 1536], P('section', 'shard'), may hold values from -0.109375 to 0.109375
- conv_weight: bfloat16 [2, 4, 3328], P('section', None, 'shard'), may hold values from -3 to 3
- conv_bias: bfloat16 [2, 3328], P('section', 'shard'), may hold values from -3 to 3
- dt_bias: bfloat16 [2, 48], P('section', 'shard'), may hold values from -6 to -2
- a_log: bfloat16 [2, 48], P('section', 'shard'), may hold values from 0 to 2.765625
- d_skip: bfloat16 [2, 48], P('section', 'shard'), may hold values from 0.5 to 1.5
- pre_gain: bfloat16 [2, 1536], P('section', 'shard'), may hold values from 0.5 to 1.5
- out_gain: bfloat16 [2, 3072], P('section', 'shard'), may hold values from 0.5 to 1.5
Outputs:
- activations: bfloat16 [2, 2, 16, 256, 1536], P('section', None, ('shard', 'rep'))
- input_grads: bfloat16 [2, 2, 16, 256, 1536], P('section', None, ('shard', 'rep'))
- grad_in_proj: float32 [2, 1536, 6400], P('section', 'shard')
- grad_dt_proj: float32 [2, 1536, 48], P('section', 'shard')
- grad_out_proj: float32 [2, 3072, 1536], P('section', 'shard')
- grad_conv_weight: float32 [2, 4, 3328], P('section', None, 'shard')
- grad_conv_bias: float32 [2, 3328], P('section', 'shard')
- grad_dt_bias: float32 [2, 48], P('section', 'shard')
- grad_a_log: float32 [2, 48], P('section', 'shard')
- grad_d_skip: float32 [2, 48], P('section', 'shard')
- grad_pre_gain: float32 [2, 1536], P('section', 'shard')
- grad_out_gain: float32 [2, 3072], P('section', 'shard')
Inputs may be any that keep to these rules, and one draw needn't show every extreme that they name: `lengths`: in each micro-batch some sequence has exactly 256 tokens.
All inputs are finite; a program needn't handle non-finite values. No bound on the sum of `lengths` on one device may be relied on, other than what follows from the above.
Results may differ from a plain program's by a relative error of at most 0.02.
Values may be sent and summed in bfloat16 or wider, within the bound.
A program may use at most 768 MiB of HBM per device.

v0:
```python
import jax
import jax.numpy as jnp
from jax import lax
from jax.sharding import PartitionSpec as P

SCAN_BLOCK = 128
HIGH = lax.Precision.HIGHEST
EPSILON = 1e-05


def from_behind(value, axis, steps):
    count = lax.axis_size(axis)
    first, last = (max(0, -steps), min(count, count - steps))
    return lax.ppermute(value, axis, [(source, source + steps) for source in range(first, last)])


def as_sent(x):

    def short(part):
        return part.astype(jnp.bfloat16) if part.dtype == jnp.float32 else part

    return jax.tree.map(short, x)


def pre_norm(rows, gain_row):
    return rows * lax.rsqrt(jnp.mean(rows * rows, axis=-1, keepdims=True) + EPSILON) * gain_row


def state_space(inputs, decay, b_rows, c_rows):
    seq_len, heads, head_dim = inputs.shape
    state_dim = b_rows.shape[1]
    blocks = seq_len // SCAN_BLOCK
    x_blocks = inputs.reshape(blocks, SCAN_BLOCK, heads, head_dim)
    d_blocks = decay.reshape(blocks, SCAN_BLOCK, heads)
    b_blocks = b_rows.reshape(blocks, SCAN_BLOCK, state_dim)
    c_blocks = c_rows.reshape(blocks, SCAN_BLOCK, state_dim)
    places = jnp.arange(SCAN_BLOCK, dtype=jnp.int32)
    lower = (places[:, None] >= places[None, :])[None, :, :]

    def advance(carried, pieces):
        x_piece, d_piece, b_piece, c_piece = pieces
        cumul = jnp.cumsum(d_piece, axis=0).T
        spread = cumul[:, :, None] - cumul[:, None, :]
        weights = jnp.where(lower, jnp.exp(jnp.where(lower, spread, 0.0)), 0.0)
        scores = jnp.dot(c_piece, b_piece.T, precision=HIGH)
        inside = jnp.einsum("hij,jhp->ihp", weights * scores[None], x_piece, precision=HIGH)
        from_state = (
            jnp.einsum("in,hpn->ihp", c_piece, carried, precision=HIGH)
            * jnp.exp(cumul).T[:, :, None]
        )
        tail = jnp.exp(cumul[:, -1:] - cumul).T
        fresh = jnp.einsum("jhp,jn->hpn", x_piece * tail[:, :, None], b_piece, precision=HIGH)
        updated = jnp.exp(cumul[:, -1])[:, None, None] * carried + fresh
        return (updated, inside + from_state)

    start = jnp.zeros((heads, head_dim, state_dim), jnp.float32)
    _, outputs = lax.scan(advance, start, (x_blocks, d_blocks, b_blocks, c_blocks))
    return outputs.reshape(seq_len, heads, head_dim)


def mixer_core(projected, dt_raw, floats):
    conv_weight, conv_bias, dt_bias, a_log, d_skip, out_gain = floats
    inner = out_gain.shape[0]
    heads = dt_bias.shape[0]
    state_dim = (conv_weight.shape[1] - inner) // 2
    taps = conv_weight.shape[0]
    seq_len = projected.shape[0]
    gate_part = projected[:, :inner]
    conv_in = projected[:, inner:]
    padded = jnp.pad(conv_in, ((taps - 1, 0), (0, 0)))
    summed = conv_bias + conv_weight[0] * padded[0:seq_len]
    for offset in range(1, taps):
        summed = summed + conv_weight[offset] * padded[offset : offset + seq_len]
    conv_act = jax.nn.silu(summed)
    x_part = conv_act[:, :inner].reshape(seq_len, heads, inner // heads)
    b_rows = conv_act[:, inner : inner + state_dim]
    c_rows = conv_act[:, inner + state_dim :]
    step_size = jax.nn.softplus(dt_raw + dt_bias)
    decay = -jnp.exp(a_log) * step_size
    output = (
        state_space(x_part * step_size[:, :, None], decay, b_rows, c_rows)
        + d_skip[None, :, None] * x_part
    )
    gated = output.reshape(seq_len, inner) * jax.nn.silu(gate_part)
    return pre_norm(gated, out_gain)


def core_floats(params):
    return tuple((params[place].astype(jnp.float32) for place in (3, 4, 5, 6, 7, 9)))


def live_mask(seq_len, count):
    return (jnp.arange(seq_len, dtype=jnp.int32) < count).astype(jnp.float32)[:, None]


def block_forward(rows, count, params):
    rows32 = rows.astype(jnp.float32)
    normed = pre_norm(rows32, params[8].astype(jnp.float32)).astype(jnp.bfloat16)
    projected = jnp.dot(normed, params[0], preferred_element_type=jnp.float32)
    dt_raw = jnp.dot(normed, params[1], preferred_element_type=jnp.float32)
    mixed = mixer_core(projected, dt_raw, core_floats(params)).astype(jnp.bfloat16)
    out_rows = jnp.dot(mixed, params[2], preferred_element_type=jnp.float32)
    result = (rows32 + live_mask(rows.shape[0], count) * out_rows).astype(jnp.bfloat16)
    return (result, (normed, projected, dt_raw, mixed))


def block_backward(cotangent, rows, stored, count, params):
    normed, projected, dt_raw, mixed = stored
    cot32 = cotangent.astype(jnp.float32)
    g_out = (cot32 * live_mask(rows.shape[0], count)).astype(jnp.bfloat16)
    d_out_proj = jnp.einsum("lk,ld->kd", mixed, g_out, preferred_element_type=jnp.float32)
    d_mixed = jnp.einsum("ld,kd->lk", g_out, params[2], preferred_element_type=jnp.float32)
    _, core_back = jax.vjp(mixer_core, projected, dt_raw, core_floats(params))
    d_projected, d_dt_raw, d_floats = core_back(d_mixed)
    d_proj_low = d_projected.astype(jnp.bfloat16)
    d_dt_low = d_dt_raw.astype(jnp.bfloat16)
    d_in_proj = jnp.einsum("ld,lk->dk", normed, d_proj_low, preferred_element_type=jnp.float32)
    d_dt_proj = jnp.einsum("ld,lk->dk", normed, d_dt_low, preferred_element_type=jnp.float32)
    d_normed = jnp.einsum(
        "lk,dk->ld", d_proj_low, params[0], preferred_element_type=jnp.float32
    ) + jnp.einsum("lk,dk->ld", d_dt_low, params[1], preferred_element_type=jnp.float32)
    _, norm_back = jax.vjp(pre_norm, rows.astype(jnp.float32), params[8].astype(jnp.float32))
    d_rows, d_pre_gain = norm_back(d_normed)
    d_input = (cot32 + d_rows).astype(jnp.bfloat16)
    grads = (
        d_in_proj,
        d_dt_proj,
        d_out_proj,
        d_floats[0],
        d_floats[1],
        d_floats[2],
        d_floats[3],
        d_floats[4],
        d_pre_gain,
        d_floats[5],
    )
    return (d_input, grads)


def add_trees(left, right):
    return tuple((a + b for a, b in zip(left, right)))


def on_device(
    boundary,
    lengths,
    in_proj,
    dt_proj,
    out_proj,
    conv_weight,
    conv_bias,
    dt_bias,
    a_log,
    d_skip,
    pre_gain,
    out_gain,
):
    section_index = lax.axis_index("section")
    shards = (
        in_proj,
        dt_proj,
        out_proj,
        conv_weight,
        conv_bias,
        dt_bias,
        a_log,
        d_skip,
        pre_gain,
        out_gain,
    )
    gathered = (
        lax.all_gather(shards[0], "shard", axis=1, tiled=True),
        lax.all_gather(shards[1], "shard", axis=1, tiled=True),
        lax.all_gather(shards[2], "shard", axis=1, tiled=True),
        lax.all_gather(shards[3], "shard", axis=2, tiled=True),
        lax.all_gather(shards[4], "shard", axis=1, tiled=True),
        lax.all_gather(shards[5], "shard", axis=1, tiled=True),
        lax.all_gather(shards[6], "shard", axis=1, tiled=True),
        lax.all_gather(shards[7], "shard", axis=1, tiled=True),
        lax.all_gather(shards[8], "shard", axis=1, tiled=True),
        lax.all_gather(shards[9], "shard", axis=1, tiled=True),
    )
    params = tuple((item[0] for item in gathered))
    own_rows = boundary[0, :, 0]
    own_counts = lengths[:, 0]
    micro = own_rows.shape[0]
    seq_len = own_rows.shape[1]
    width = own_rows.shape[2]

    def zero_stored():
        return (
            jnp.zeros((seq_len, width), jnp.bfloat16),
            jnp.zeros((seq_len, params[0].shape[1]), jnp.float32),
            jnp.zeros((seq_len, params[1].shape[1]), jnp.float32),
            jnp.zeros((seq_len, params[2].shape[0]), jnp.bfloat16),
        )

    def run_forward(rows, count):
        return block_forward(rows, count, params)

    def spare_forward(rows, count):
        return (jnp.zeros((seq_len, width), jnp.bfloat16), zero_stored())

    incoming = jnp.zeros((seq_len, width), jnp.bfloat16)
    outputs = jnp.zeros((micro, seq_len, width), jnp.bfloat16)
    saved = []
    for moment in range(micro + 1):
        micro_index = moment - section_index
        active = (micro_index >= 0) & (micro_index < micro)
        slot_index = jnp.clip(micro_index, 0, micro - 1)
        block_in = jnp.where(
            section_index == 0, lax.dynamic_index_in_dim(own_rows, slot_index, 0, False), incoming
        )
        count = lax.dynamic_index_in_dim(own_counts, slot_index, 0, False)
        result, stored = lax.cond(active, run_forward, spare_forward, block_in, count)
        outputs = jnp.where(
            active, lax.dynamic_update_index_in_dim(outputs, result, slot_index, 0), outputs
        )
        saved.append((block_in, stored, count, active, slot_index))
        if moment < micro:
            incoming = from_behind(result, "section", 1)
    regathered = (
        lax.all_gather(shards[0], "shard", axis=1, tiled=True),
        lax.all_gather(shards[1], "shard", axis=1, tiled=True),
        lax.all_gather(shards[2], "shard", axis=1, tiled=True),
        lax.all_gather(shards[3], "shard", axis=2, tiled=True),
        lax.all_gather(shards[4], "shard", axis=1, tiled=True),
        lax.all_gather(shards[5], "shard", axis=1, tiled=True),
        lax.all_gather(shards[6], "shard", axis=1, tiled=True),
        lax.all_gather(shards[7], "shard", axis=1, tiled=True),
        lax.all_gather(shards[8], "shard", axis=1, tiled=True),
        lax.all_gather(shards[9], "shard", axis=1, tiled=True),
    )
    back_params = tuple((item[0] for item in regathered))

    def run_backward(cotangent, rows, stored, count):
        return block_backward(cotangent, rows, stored, count, back_params)

    def spare_backward(cotangent, rows, stored, count):
        return (
            jnp.zeros((seq_len, width), jnp.bfloat16),
            tuple((jnp.zeros(item.shape, jnp.float32) for item in back_params)),
        )

    incoming_grad = jnp.zeros((seq_len, width), jnp.bfloat16)
    in_grads = jnp.zeros((micro, seq_len, width), jnp.bfloat16)
    total = None
    for moment in range(micro + 1):
        block_in, stored, count, active, slot_index = saved[micro - moment]
        cotangent = jnp.where(
            section_index == 1,
            lax.dynamic_index_in_dim(own_rows, slot_index, 0, False),
            incoming_grad,
        )
        d_input, grads = lax.cond(
            active, run_backward, spare_backward, cotangent, block_in, stored, count
        )
        in_grads = jnp.where(
            active, lax.dynamic_update_index_in_dim(in_grads, d_input, slot_index, 0), in_grads
        )
        if moment < micro:
            incoming_grad = from_behind(d_input, "section", -1)
        total = grads if total is None else add_trees(total, grads)
    owned = (
        lax.psum_scatter(
            total[0].astype(jnp.bfloat16), "shard", scatter_dimension=0, tiled=True
        ).astype(jnp.float32),
        lax.psum_scatter(
            total[1].astype(jnp.bfloat16), "shard", scatter_dimension=0, tiled=True
        ).astype(jnp.float32),
        lax.psum_scatter(
            total[2].astype(jnp.bfloat16), "shard", scatter_dimension=0, tiled=True
        ).astype(jnp.float32),
        lax.psum_scatter(
            total[3].astype(jnp.bfloat16), "shard", scatter_dimension=1, tiled=True
        ).astype(jnp.float32),
        lax.psum_scatter(
            total[4].astype(jnp.bfloat16), "shard", scatter_dimension=0, tiled=True
        ).astype(jnp.float32),
        lax.psum_scatter(
            total[5].astype(jnp.bfloat16), "shard", scatter_dimension=0, tiled=True
        ).astype(jnp.float32),
        lax.psum_scatter(
            total[6].astype(jnp.bfloat16), "shard", scatter_dimension=0, tiled=True
        ).astype(jnp.float32),
        lax.psum_scatter(
            total[7].astype(jnp.bfloat16), "shard", scatter_dimension=0, tiled=True
        ).astype(jnp.float32),
        lax.psum_scatter(
            total[8].astype(jnp.bfloat16), "shard", scatter_dimension=0, tiled=True
        ).astype(jnp.float32),
        lax.psum_scatter(
            total[9].astype(jnp.bfloat16), "shard", scatter_dimension=0, tiled=True
        ).astype(jnp.float32),
    )
    summed = jax.tree.map(lambda part: part.astype(jnp.float32), lax.psum(as_sent(owned), "rep"))
    final = tuple((item[None] for item in summed))
    return (
        outputs[None, :, None],
        in_grads[None, :, None],
        final[0],
        final[1],
        final[2],
        final[3],
        final[4],
        final[5],
        final[6],
        final[7],
        final[8],
        final[9],
    )


def solution(mesh):
    in_specs = (
        P("section", None, ("shard", "rep"), None, None),
        P(None, ("shard", "rep")),
        P("section", "shard", None),
        P("section", "shard", None),
        P("section", "shard", None),
        P("section", None, "shard"),
        P("section", "shard"),
        P("section", "shard"),
        P("section", "shard"),
        P("section", "shard"),
        P("section", "shard"),
        P("section", "shard"),
    )
    out_specs = (
        P("section", None, ("shard", "rep"), None, None),
        P("section", None, ("shard", "rep"), None, None),
        P("section", "shard", None),
        P("section", "shard", None),
        P("section", "shard", None),
        P("section", None, "shard"),
        P("section", "shard"),
        P("section", "shard"),
        P("section", "shard"),
        P("section", "shard"),
        P("section", "shard"),
        P("section", "shard"),
    )
    return jax.shard_map(
        on_device, mesh=mesh, in_specs=in_specs, out_specs=out_specs, check_vma=False
    )
```

profile of v0, /device:TPU:0, one launch (start us, length us, event | category | flops | bytes accessed | tf_op | source)
XLA Modules:
  0.0 2693.9 jit_solution(14970451352565655027)
XLA Ops:
  12.0 57.2 %all_gather.41 = bf16[1,4,3328]{1,0,2:T(2,128)(2,1)S(1)} all-gather(bf16[1,4,832]{1,0,2:T(2,128)(2,1)} %copy.733), channel_id=1, replica_groups=mesh['section'=2,'shard'=4,'rep'=4] {'shard'}, dimensions={2}, use_global_device_ids=true | all-gather | bytes 33280 | tf_op jit(solution)/shard_map/all_gather | solution.py:175
  71.0 18.8 all_gather.48
  89.9 14.1 all_gather.42
  118.8 26.5 all_gather.44
  146.3 59.6 %all-gather.5.cloned.1.call-done = bf16[1,3072,1536]{2,1,0:T(8,128)(2,1)} async-done(((bf16[1,768,1536]{2,1,0:T(8,128)(2,1)}), bf16[1,3072,1536]{2,1,0:T(8,128)(2,1)}) %all-gather.5.cloned.1.call-update) | async-done | bytes 9437200 | tf_op jit(solution)/shard_map/all_gather | solution.py:174
  205.8 336.6 %all-gather.3.cloned.1.call-done = bf16[1,1536,6400]{2,1,0:T(8,128)(2,1)} async-done(((bf16[1,384,6400]{2,1,0:T(8,128)(2,1)}), bf16[1,1536,6400]{2,1,0:T(8,128)(2,1)}) %all-gather.3.cloned.1.call-update) | async-done | bytes 19660816 | tf_op jit(solution)/shard_map/all_gather | solution.py:172
  542.4 112.4 %conditional.6 = (bf16[256,1536]{1,0:T(8,128)(2,1)}, bf16[256,1536]{1,0:T(8,128)(2,1)}, f32[256,6400]{1,0:T(8,128)}, f32[256,48]{0,1:T(8,128)}, bf16[256,3072]{1...) conditional(s32[]{:T(128)} %convert_element_type.338, () %tuple.200, (bf16[256,1536]{1,0:T(8,128)(2,1)S(1)}, s32[]{:T(128)}, ...), branch_computations={%region_0.1_spmd, %region_1.7_spmd} | conditional | flops 9355532288 | bytes 165452624 | solution.py:215
  583.5 43.0 %while.240 = (s32[]{:T(128)}, f32[48,64,128]{2,1,0:T(8,128)S(1)}, f32[2,128,48,64]{1,3,2,0:T(8,128)}, f32[2,128,48]{2,1,0:T(8,128)S(1)}, f32[2,128,48,64]{1,0,3,...) while((s32[]{:T(128)}, f32[48,64,128]{2,1,0:T(8,128)S(1)}, ...), condition=%wide.region_5.5_spmd.clone.clone, body=%wide.region_3.4_spmd.clone.clone.sunk | while | flops 1843806208 | bytes 17469076 | solution.py:57
  661.3 113.3 %conditional.7 = (bf16[256,1536]{1,0:T(8,128)(2,1)}, bf16[256,1536]{1,0:T(8,128)(2,1)}, f32[256,6400]{1,0:T(8,128)}, f32[256,48]{0,1:T(8,128)}, bf16[256,3072]{1...) conditional(s32[]{:T(128)} %convert_element_type.339, () %tuple.202, (bf16[256,1536]{1,0:T(8,128)(2,1)S(1)}, s32[]{:T(128)}, ...), branch_computations={%region_7.8_spmd, %region_8.14_spmd} | conditional | flops 9355532288 | bytes 165452624 | solution.py:215
  703.2 43.2 %while.241 = (s32[]{:T(128)}, f32[48,64,128]{2,1,0:T(8,128)S(1)}, f32[2,128,48,64]{1,3,2,0:T(8,128)}, f32[2,128,48]{2,1,0:T(8,128)S(1)}, f32[2,128,48,64]{1,0,3,...) while((s32[]{:T(128)}, f32[48,64,128]{2,1,0:T(8,128)S(1)}, ...), condition=%wide.region_12.12_spmd.clone.clone, body=%wide.region_10.11_spmd.clone.clone.sunk | while | flops 1843806208 | bytes 17469076 | solution.py:57
  793.3 32.9 %conditional.9 = (bf16[256,1536]{1,0:T(8,128)(2,1)}, f32[1536,48]{0,1:T(8,128)}, f32[4,3328]{1,0:T(4,128)}, f32[3328]{0:T(1024)}, f32[48]{0:T(128)}, /*index=5*/...) conditional(s32[]{:T(128)} %convert_element_type.340, ...), branch_computations={%region_21.22_spmd, %region_22.0_spmd} | conditional | flops 20592838656 | bytes 814240640 | solution.py:255
  827.5 422.0 %collective-permute-done.2 = bf16[256,1536]{1,0:T(8,128)(2,1)S(1)} collective-permute-done((bf16[256,1536]{1,0:T(8,128)(2,1)}, bf16[256,1536]{1,0:T(8,128)(2,1)S(1)}, u32[]{:S(2)}, u32[]{:S(2)}) %collective-permute-start.2) | collective-permute-done | bytes 786464 | tf_op jit(solution)/shard_map/ppermute | solution.py:14
  1249.5 352.6 %conditional.10 = (bf16[256,1536]{1,0:T(8,128)(2,1)}, f32[1536,48]{0,1:T(8,128)}, f32[4,3328]{1,0:T(4,128)}, f32[3328]{0:T(1024)}, f32[48]{0:T(128)}, /*index=5*...) conditional(s32[]{:T(128)} %convert_element_type.339, ...), branch_computations={%region_52.54_spmd, %region_53.84_spmd} | conditional | flops 20592838656 | bytes 781147136 | solution.py:255
  1283.1 60.2 %while.245 = (s32[]{:T(128)}, f32[48,64,128]{2,1,0:T(8,128)S(1)}, f32[2,128,48,64]{1,3,2,0:T(8,128)}, f32[2,48,128,128]{3,2,1,0:T(8,128)}, f32[2,128,128]{1,2,0:...) while((s32[]{:T(128)}, f32[48,64,128]{2,1,0:T(8,128)S(1)}, ...), condition=%wide.region_56.57_spmd.clone.clone, body=%wide.region_54.56_spmd.clone.clone.sunk | while | flops 1847734272 | bytes 84601144 | solution.py:57
  1389.8 68.0 %while.246 = (s32[]{:T(128)}, f32[48,64,128]{2,1,0:T(8,128)S(1)}, f32[2,128,48,64]{1,3,2,0:T(8,128)}, f32[2,128,48]{2,1,0:T(8,128)S(1)}, f32[2,128,128]{2,1,0:T(...) while((s32[]{:T(128)}, f32[48,64,128]{2,1,0:T(8,128)S(1)}, ...), condition=%wide.region_68.69_spmd.clone.clone, body=%wide.region_59.68_spmd.clone.clone.sunk | while | flops 3687632896 | bytes 91598432 | solution.py:57
  1489.6 17.5 convolution_bitcast_fusion.3
  1507.1 39.4 %copy.772 = f32[1536,6400]{1,0:T(8,128)} copy(f32[1536,6400]{0,1:T(8,128)} %convolution_bitcast_fusion.3) | data formatting | bytes 78643200 | tf_op jit(solution)/shard_map/cond | solution.py:255
  1583.4 18.7 copy.774
  1606.5 350.7 %conditional.11 = (f32[1536,48]{0,1:T(8,128)}, f32[4,3328]{1,0:T(4,128)}, f32[3328]{0:T(1024)}, f32[48]{0:T(128)}, f32[48]{0:T(128)}, /*index=5*/f32[48]{0:T(128...) conditional(s32[]{:T(128)} %convert_element_type.338, ...), branch_computations={%region_83.85_spmd, %region_84.115_spmd} | conditional | flops 20592838656 | bytes 793205952 | solution.py:255
  1640.2 60.4 %while.247 = (s32[]{:T(128)}, f32[48,64,128]{2,1,0:T(8,128)S(1)}, f32[2,128,48,64]{1,3,2,0:T(8,128)}, f32[2,48,128,128]{3,2,1,0:T(8,128)}, f32[2,128,128]{1,2,0:...) while((s32[]{:T(128)}, f32[48,64,128]{2,1,0:T(8,128)S(1)}, ...), condition=%wide.region_87.88_spmd.clone.clone, body=%wide.region_85.87_spmd.clone.clone.sunk | while | flops 1847734272 | bytes 84601144 | solution.py:57
  1747.5 68.0 %while.248 = (s32[]{:T(128)}, f32[48,64,128]{2,1,0:T(8,128)S(1)}, f32[2,128,48,64]{1,3,2,0:T(8,128)}, f32[2,128,48]{2,1,0:T(8,128)S(1)}, f32[2,128,128]{2,1,0:T(...) while((s32[]{:T(128)}, f32[48,64,128]{2,1,0:T(8,128)S(1)}, ...), condition=%wide.region_99.100_spmd.clone.clone, body=%wide.region_90.99_spmd.clone.clone.sunk | while | flops 3687632896 | bytes 91598432 | solution.py:57
  1847.0 17.4 convolution_bitcast_fusion.6
  1864.4 39.6 %copy.776 = f32[1536,6400]{1,0:T(8,128)} copy(f32[1536,6400]{0,1:T(8,128)} %convolution_bitcast_fusion.6) | data formatting | bytes 78643200 | tf_op jit(solution)/shard_map/cond | solution.py:255
  1938.4 18.6 copy.778
  1957.2 22.4 add_convert_fusion.10
  1979.7 44.0 %add_convert_fusion.9 = bf16[1536,6400]{1,0:T(8,128)(2,1)} fusion(f32[1536,6400]{1,0:T(8,128)} %get-tuple-element.5079, f32[1536,6400]{1,0:T(8,128)} %get-tuple-element.5075, f32[1536,6400]{1,0:T(8,128)} %get-tuple-element.5077), kind=kLoop, calls=%fused_computation.929 | loop fusion | flops 29491200 | bytes 137625600 | tf_op jit(solution)/shard_map/convert_element_type | solution.py:266
  2028.2 111.5 %reduce-scatter.11.cloned.1.call-done = bf16[768,1536]{1,0:T(8,128)(2,1)} async-done(((bf16[3072,1536]{1,0:T(8,128)(2,1)}), bf16[768,1536]{1,0:T(8,128)(2,1)}) %reduce-scatter.11.cloned.1.call-update) | async-done | bytes 2359312 | tf_op jit(solution)/shard_map/reduce_scatter | solution.py:271
  2139.7 329.7 %reduce-scatter.9.cloned.1.call-done = bf16[384,6400]{1,0:T(8,128)(2,1)} async-done(((bf16[1536,6400]{1,0:T(8,128)(2,1)}), bf16[384,6400]{1,0:T(8,128)(2,1)}) %reduce-scatter.9.cloned.1.call-update) | async-done | bytes 4915216 | tf_op jit(solution)/shard_map/reduce_scatter | solution.py:265
  2481.3 19.3 all-reduce.63
  2503.8 16.3 reduce-scatter.13.cloned.1.call-done
  2521.1 18.2 all-reduce.61
  2543.8 133.1 %all-reduce.67.cloned.1.call-done = (bf16[1,384,6400]{2,1,0:T(8,128)(2,1)}, bf16[1,768,1536]{2,1,0:T(8,128)(2,1)}) async-done(((bf16[1,384,6400]{2,1,0:T(8,128)(2,1)}, bf16[1,768,1536]{2,1,0:T(8,128)(2,1)}), (bf16[1,384,6400]{2,1,0:T(8,128)(2,1)}, bf16[1,768,1536]{2,1,0:T(8,128)(2,1)})) %all-reduce.67.cloned.1.call-update) | async-done | bytes 7274512 | tf_op jit(solution)/shard_map/psum | solution.py:296
  (1128 shorter events, 887.5 us)
Async XLA Ops:
  7.2 198.6 %all-gather.5.cloned.1.call-start = ((), (), s32[]{:S(2)}) async-start(), calls=%async_computation.5 | async-start | bytes 11796480 | tf_op jit(solution)/shard_map/all_gather | solution.py:174
  7.9 534.5 %all-gather.3.cloned.1.call-start = ((), (), s32[]{:S(2)}) async-start(), calls=%async_computation.4 | async-start | bytes 24576000 | tf_op jit(solution)/shard_map/all_gather | solution.py:172
  8.7 62.1 %copy-start.253 = (bf16[1,384,48]{1,2,0:T(8,128)(2,1)S(1)}, bf16[1,384,48]{1,2,0:T(8,128)(2,1)}, u32[]{:S(2)}) copy-start(bf16[1,384,48]{1,2,0:T(8,128)(2,1)} %param.46) | copy-start | bytes 110596
  8.7 62.2 %copy-start.277 = (bf16[1,832]{1,0:T(2,128)(2,1)S(1)}, bf16[1,832]{1,0:T(2,128)(2,1)}, u32[]{:S(2)}) copy-start(bf16[1,832]{1,0:T(2,128)(2,1)} %param.49) | copy-start | bytes 4996
  8.7 62.3 %copy-start.278 = (bf16[1,768]{1,0:T(2,128)(2,1)S(1)}, bf16[1,768]{1,0:T(2,128)(2,1)}, u32[]{:S(2)}) copy-start(bf16[1,768]{1,0:T(2,128)(2,1)} %param.54) | copy-start | bytes 4612
  8.7 81.1 %copy-start.292 = (bf16[1,384]{1,0:T(2,128)(2,1)S(1)}, bf16[1,384]{1,0:T(2,128)(2,1)}, u32[]{:S(2)}) copy-start(bf16[1,384]{1,0:T(2,128)(2,1)} %param.53) | copy-start | bytes 2308
  8.7 95.3 %copy-start.293 = (bf16[1,12]{1,0:T(2,128)(2,1)S(1)}, bf16[1,12]{1,0:T(2,128)(2,1)}, u32[]{:S(2)}) copy-start(bf16[1,12]{1,0:T(2,128)(2,1)} %param.51) | copy-start | bytes 76
  8.7 95.6 %copy-start.294 = (bf16[1,12]{1,0:T(2,128)(2,1)S(1)}, bf16[1,12]{1,0:T(2,128)(2,1)}, u32[]{:S(2)}) copy-start(bf16[1,12]{1,0:T(2,128)(2,1)} %param.52) | copy-start | bytes 76
  8.7 95.8 %copy-start.295 = (bf16[1,12]{1,0:T(2,128)(2,1)S(1)}, bf16[1,12]{1,0:T(2,128)(2,1)}, u32[]{:S(2)}) copy-start(bf16[1,12]{1,0:T(2,128)(2,1)} %param.50) | copy-start | bytes 76
  8.8 96.2 %copy-start.276 = (s32[2,1]{0,1:T(1,128)S(1)}, s32[2,1]{0,1:T(1,128)}, u32[]{:S(2)}) copy-start(s32[2,1]{0,1:T(1,128)} %param.44) | copy-start | bytes 28
  8.8 136.5 %copy-start.97 = (bf16[1,2,1,256,1536]{4,3,2,1,0:T(8,128)(2,1)S(1)}, bf16[1,2,1,256,1536]{4,3,2,1,0:T(8,128)(2,1)}, u32[]{:S(2)}) copy-start(bf16[1,2,1,256,1536]{4,3,2,1,0:T(8,128)(2,1)} %param.43) | copy-start | bytes 4718596
  8.8 2130.9 %reduce-scatter.11.cloned.1.call-start = ((), (), s32[]{:S(2)}) async-start(), calls=%async_computation.7 | async-start | bytes 11796480 | tf_op jit(solution)/shard_map/reduce_scatter | solution.py:271
  70.8 471.6 %copy-start.120 = (bf16[1,4,3328]{2,1,0:T(4,128)(2,1)}, bf16[1,4,3328]{2,1,0:T(4,128)(2,1)S(1)}, u32[]{:S(2)}) copy-start(bf16[1,4,3328]{2,1,0:T(4,128)(2,1)S(1)} %copy.734) | copy-start | bytes 79876
  89.9 703.4 %copy-start.181 = (bf16[3072]{0:T(1024)(128)(2,1)}, bf16[3072]{0:T(1024)(128)(2,1)S(1)}, u32[]{:S(2)}) copy-start(bf16[3072]{0:T(1024)(128)(2,1)S(1)} %reduce.32) | copy-start | bytes 18436
  104.0 438.4 %copy-start.193 = (bf16[1536]{0:T(1024)(128)(2,1)}, bf16[1536]{0:T(1024)(128)(2,1)S(1)}, u32[]{:S(2)}) copy-start(bf16[1536]{0:T(1024)(128)(2,1)S(1)} %reduce.31) | copy-start | bytes 9220
  118.8 423.7 %copy-start.296 = (bf16[48]{0:T(256)(128)(2,1)}, bf16[48]{0:T(256)(128)(2,1)S(1)}, u32[]{:S(2)}) copy-start(bf16[48]{0:T(256)(128)(2,1)S(1)} %get-tuple-element.5482) | copy-start | bytes 292
  118.8 423.7 %copy-start.302 = (bf16[48]{0:T(256)(128)(2,1)}, bf16[48]{0:T(256)(128)(2,1)S(1)}, u32[]{:S(2)}) copy-start(bf16[48]{0:T(256)(128)(2,1)S(1)} %get-tuple-element.5483) | copy-start | bytes 292
  118.8 674.5 %copy-start.186 = (bf16[3328]{0:T(1024)(128)(2,1)}, bf16[3328]{0:T(1024)(128)(2,1)S(1)}, u32[]{:S(2)}) copy-start(bf16[3328]{0:T(1024)(128)(2,1)S(1)} %get-tuple-element.5481) | copy-start | bytes 19972
  146.3 396.2 %copy-start.52 = (bf16[256,1536]{1,0:T(8,128)(2,1)}, bf16[256,1536]{1,0:T(8,128)(2,1)S(1)}, u32[]{:S(2)}) copy-start(bf16[256,1536]{1,0:T(8,128)(2,1)S(1)} %get-tuple-element.5529) | copy-start | bytes 2359300
  654.8 3.4 collective-permute-start
  774.6 4.5 collective-permute-start.1
  826.2 423.3 %collective-permute-start.2 = (bf16[256,1536]{1,0:T(8,128)(2,1)}, bf16[256,1536]{1,0:T(8,128)(2,1)S(1)}, u32[]{:S(2)}, u32[]{:S(2)}) collective-permute-start(bf16[256,1536]{1,0:T(8,128)(2,1)} %get-tuple-element.2930), channel_id=1, source_target_pairs={{16,0},{17,1},{18,2},{19,3},{20,4},{21,5},{22,6},{23,7},{24,8},{25... | collective-permute-start | bytes 2359304 | tf_op jit(solution)/shard_map/ppermute | solution.py:14
  1507.1 39.5 %copy-start.154 = (f32[2,128,48]{2,1,0:T(8,128)S(1)}, f32[2,128,48]{2,1,0:T(8,128)}, u32[]{:S(2)}) copy-start(f32[2,128,48]{2,1,0:T(8,128)} %copy-done.153) | copy-start | bytes 147460 | tf_op jit(solution)/shard_map/cond
  1507.1 40.2 %copy-start.45 = (f32[256,3072]{0,1:T(8,128)S(1)}, f32[256,3072]{0,1:T(8,128)}, u32[]{:S(2)}) copy-start(f32[256,3072]{0,1:T(8,128)} %copy.686) | copy-start | bytes 9437188 | tf_op jit(solution)/shard_map/cond
  1602.1 4.4 collective-permute-start.3
  1864.4 39.6 %copy-start.156 = (f32[2,128,48]{2,1,0:T(8,128)S(1)}, f32[2,128,48]{2,1,0:T(8,128)}, u32[]{:S(2)}) copy-start(f32[2,128,48]{2,1,0:T(8,128)} %copy-done.155) | copy-start | bytes 147460 | tf_op jit(solution)/shard_map/cond
  1864.4 40.3 %copy-start.46 = (f32[256,3072]{0,1:T(8,128)S(1)}, f32[256,3072]{0,1:T(8,128)}, u32[]{:S(2)}) copy-start(f32[256,3072]{0,1:T(8,128)} %copy.715) | copy-start | bytes 9437188 | tf_op jit(solution)/shard_map/cond
  1979.6 489.8 %reduce-scatter.9.cloned.1.call-start = ((), (), s32[]{:S(2)}) async-start(), calls=%async_computation.6 | async-start | bytes 24576000 | tf_op jit(solution)/shard_map/reduce_scatter | solution.py:265
  2023.7 478.8 %reduce-scatter.15.cloned.1.call-start = ((), (), s32[]{:S(2)}) async-start(), calls=%async_computation.9 | async-start | bytes 1064960
  2025.9 494.1 %reduce-scatter.13.cloned.1.call-start = ((), (), s32[]{:S(2)}) async-start(), calls=%async_computation.8 | async-start | bytes 491520
  2028.1 648.8 %all-reduce.67.cloned.1.call-start = ((), (), s32[]{:S(2)}) async-start(), calls=%async_computation.10 | async-start | bytes 14548992 | tf_op jit(solution)/shard_map/psum | solution.py:296
  2502.5 181.5 %copy-start.118 = (bf16[1,2,1,256,1536]{4,3,2,1,0:T(8,128)(2,1)}, bf16[1,2,1,256,1536]{4,3,2,1,0:T(8,128)(2,1)S(1)}, u32[]{:S(2)}) copy-start(bf16[1,2,1,256,1536]{4,3,2,1,0:T(8,128)(2,1)S(1)} %bitcast_dynamic-update-slice_fusion.28) | copy-start | bytes 4718596
  (261 other events, 984.8 us)
Sparse Core Ops, SparseCore 0:
  9.6 196.2 all-gather.4
  207.4 334.9 all-gather.2
  1979.7 159.9 reduce-scatter.10
  2141.9 327.4 reduce-scatter.8
  2472.1 26.1 reduce-scatter.14
  2500.5 19.5 reduce-scatter.12
  2523.7 153.1 all-reduce.66
where the time goes:
time: 2710 us; the launch traced here: 2690 us
  waiting for transfers between devices  1420 us (52%)
  local copies, waits for them, and re-layouts  430 us (16%)
  matrix products  378 us (14%)
  other arithmetic  259 us (10%)
  blocking collectives  167 us (6%)
    ppermute x4, waiting for transfers between devices, from_behind(): lax.ppermute(value, axis, [(source, source + steps) for source in range(f...  429 us
    all_gather x1, waiting for transfers between devices, on_device(): lax.all_gather(shards[0], 'shard', axis=1, tiled=True)  337 us
    reduce_scatter x1, waiting for transfers between devices, on_device(): lax.psum_scatter(total[0].astype(jnp.bfloat16), 'shard', scatter_dimensio...  330 us
    psum x1, waiting for transfers between devices, on_device(): lax.psum(as_sent(owned), 'rep')  133 us
    dot_general x16, matrix products, advance(): jnp.einsum('hij,jhp->ihp', weights * scores[None], x_piece, precision=HIGH)  125 us
    cond x4, local copies, waits for them, and re-layouts, on_device(): lax.cond(active, run_backward, spare_backward, cotangent, block_in, store...  116 us
    reduce_scatter x1, waiting for transfers between devices, on_device(): lax.psum_scatter(total[2].astype(jnp.bfloat16), 'shard', scatter_dimensio...  112 us
    all_gather x1, waiting for transfers between devices, on_device(): lax.all_gather(shards[2], 'shard', axis=1, tiled=True)  59.6 us
  transfers between devices with their start and end apart: 11, of which 10 were waited for; matrix products, arithmetic and copies ran while one was open for 3% of the time, Pallas kernels for 0%

commit v1 on v0

--- a/solution.py
+++ b/solution.py
@@ -169,7 +169,7 @@
         out_gain,
     )
     gathered = (
-        lax.all_gather(shards[0], "shard", axis=1, tiled=True),
+        jnp.concatenate(lax.all_gather(shards[0], "shard"), axis=1),
         lax.all_gather(shards[1], "shard", axis=1, tiled=True),
         lax.all_gather(shards[2], "shard", axis=1, tiled=True),
         lax.all_gather(shards[3], "shard", axis=2, tiled=True),

time: 2710 us -> 2710 us (level)
    all_gather x0 -> x1, waiting for transfers between devices: none -> 336 us  [on_device(): lax.all_gather(shards[0], 'shard')]
    all_gather x1, waiting for transfers between devices: 337 us -> 81.5 us  [on_device(): lax.all_gather(shards[0], 'shard', axis=1, tiled=True)]
    ppermute x4, waiting for transfers between devices: 429 us -> 347 us  [from_behind(): lax.ppermute(value, axis, [(source, source + steps) for source in range(f...]
  transfers between devices with their start and end apart: 11 -> 12, of which waited for: 10 -> 11; matrix products, arithmetic and copies ran while one was open for 3% -> 11% of each run, Pallas kernels for 0% -> 0%
where the time goes in v1:
time: 2710 us; the launch traced here: 2700 us
  waiting for transfers between devices  1420 us (52%)
  local copies, waits for them, and re-layouts  433 us (16%)
  matrix products  379 us (14%)
  other arithmetic  259 us (10%)
  blocking collectives  167 us (6%)
    ppermute x4, waiting for transfers between devices, from_behind(): lax.ppermute(value, axis, [(source, source + steps) for source in range(f...  347 us
    all_gather x1, waiting for transfers between devices, on_device(): lax.all_gather(shards[0], 'shard')  336 us
    reduce_scatter x1, waiting for transfers between devices, on_device(): lax.psum_scatter(total[0].astype(jnp.bfloat16), 'shard', scatter_dimensio...  330 us
    psum x1, waiting for transfers between devices, on_device(): lax.psum(as_sent(owned), 'rep')  133 us
    dot_general x16, matrix products, advance(): jnp.einsum('hij,jhp->ihp', weights * scores[None], x_piece, precision=HIGH)  125 us
    cond x4, local copies, waits for them, and re-layouts, on_device(): lax.cond(active, run_backward, spare_backward, cotangent, block_in, store...  116 us
    reduce_scatter x1, waiting for transfers between devices, on_device(): lax.psum_scatter(total[2].astype(jnp.bfloat16), 'shard', scatter_dimensio...  111 us
    all_gather x1, waiting for transfers between devices, on_device(): lax.all_gather(shards[0], 'shard', axis=1, tiled=True)  81.5 us
  transfers between devices with their start and end apart: 12, of which 11 were waited for; matrix products, arithmetic and copies ran while one was open for 11% of the time, Pallas kernels for 0%

profile of v1, /device:TPU:0, one launch (start us, length us, event | category | flops | bytes accessed | tf_op | source)
XLA Modules:
  0.0 2697.7 jit_solution(12896643691691952317)
XLA Ops:
  12.6 57.8 %all_gather.46 = bf16[1,4,3328]{1,0,2:T(2,128)(2,1)S(1)} all-gather(bf16[1,4,832]{1,0,2:T(2,128)(2,1)} %copy.733), channel_id=1, replica_groups=mesh['section'=2,'shard'=4,'rep'=4] {'shard'}, dimensions={2}, use_global_device_ids=true | all-gather | bytes 33280 | tf_op jit(solution)/shard_map/all_gather | solution.py:175
  72.3 18.2 all_gather.54
  119.5 25.9 all_gather.50
  146.5 60.0 %all-gather.5.cloned.1.call-done = bf16[1,3072,1536]{2,1,0:T(8,128)(2,1)} async-done(((bf16[1,768,1536]{2,1,0:T(8,128)(2,1)}), bf16[1,3072,1536]{2,1,0:T(8,128)(2,1)}) %all-gather.5.cloned.1.call-update) | async-done | bytes 9437200 | tf_op jit(solution)/shard_map/all_gather | solution.py:174
  206.5 336.4 %all-gather.9.cloned.1.call-done = bf16[4,384,6400]{2,1,0:T(8,128)(2,1)} async-done(((bf16[1,384,6400]{2,1,0:T(8,128)(2,1)}), bf16[4,384,6400]{2,1,0:T(8,128)(2,1)}) %all-gather.9.cloned.1.call-update) | async-done | bytes 19660816 | tf_op jit(solution)/shard_map/all_gather | solution.py:172
  543.0 113.7 %conditional.6 = (bf16[256,1536]{1,0:T(8,128)(2,1)}, bf16[256,1536]{1,0:T(8,128)(2,1)}, f32[256,6400]{1,0:T(8,128)}, f32[256,48]{0,1:T(8,128)}, bf16[256,3072]{1...) conditional(s32[]{:T(128)} %convert_element_type.338, () %tuple.200, (bf16[256,1536]{1,0:T(8,128)(2,1)S(1)}, s32[]{:T(128)}, ...), branch_computations={%region_0.1_spmd, %region_1.7_spmd} | conditional | flops 9355532288 | bytes 165452624 | solution.py:215
  585.3 42.9 %while.240 = (s32[]{:T(128)}, f32[48,64,128]{2,1,0:T(8,128)S(1)}, f32[2,128,48,64]{1,3,2,0:T(8,128)}, f32[2,128,48]{2,1,0:T(8,128)S(1)}, f32[2,128,48,64]{1,0,3,...) while((s32[]{:T(128)}, f32[48,64,128]{2,1,0:T(8,128)S(1)}, ...), condition=%wide.region_5.5_spmd.clone.clone, body=%wide.region_3.4_spmd.clone.clone.sunk | while | flops 1843806208 | bytes 17469076 | solution.py:57
  663.1 113.7 %conditional.7 = (bf16[256,1536]{1,0:T(8,128)(2,1)}, bf16[256,1536]{1,0:T(8,128)(2,1)}, f32[256,6400]{1,0:T(8,128)}, f32[256,48]{0,1:T(8,128)}, bf16[256,3072]{1...) conditional(s32[]{:T(128)} %convert_element_type.339, () %tuple.202, (bf16[256,1536]{1,0:T(8,128)(2,1)S(1)}, s32[]{:T(128)}, ...), branch_computations={%region_7.8_spmd, %region_8.14_spmd} | conditional | flops 9355532288 | bytes 165452624 | solution.py:215
  705.2 43.2 %while.241 = (s32[]{:T(128)}, f32[48,64,128]{2,1,0:T(8,128)S(1)}, f32[2,128,48,64]{1,3,2,0:T(8,128)}, f32[2,128,48]{2,1,0:T(8,128)S(1)}, f32[2,128,48,64]{1,0,3,...) while((s32[]{:T(128)}, f32[48,64,128]{2,1,0:T(8,128)S(1)}, ...), condition=%wide.region_12.12_spmd.clone.clone, body=%wide.region_10.11_spmd.clone.clone.sunk | while | flops 1843806208 | bytes 17469076 | solution.py:57
  797.2 81.5 %all-gather.7.cloned.1.call-done = bf16[1,1536,6400]{2,1,0:T(8,128)(2,1)} async-done(((bf16[1,384,6400]{2,1,0:T(8,128)(2,1)}), bf16[1,1536,6400]{2,1,0:T(8,128)(2,1)}) %all-gather.7.cloned.1.call-update) | async-done | bytes 19660816 | tf_op jit(solution)/shard_map/all_gather | solution.py:223
  879.7 32.9 %conditional.9 = (bf16[256,1536]{1,0:T(8,128)(2,1)}, f32[1536,48]{0,1:T(8,128)}, f32[4,3328]{1,0:T(4,128)}, f32[3328]{0:T(1024)}, f32[48]{0:T(128)}, /*index=5*/...) conditional(s32[]{:T(128)} %convert_element_type.340, ...), branch_computations={%region_21.22_spmd, %region_22.0_spmd} | conditional | flops 20592838656 | bytes 777999360 | solution.py:255
  913.9 339.3 %collective-permute-done.2 = bf16[256,1536]{1,0:T(8,128)(2,1)S(1)} collective-permute-done((bf16[256,1536]{1,0:T(8,128)(2,1)}, bf16[256,1536]{1,0:T(8,128)(2,1)S(1)}, u32[]{:S(2)}, u32[]{:S(2)}) %collective-permute-start.2) | collective-permute-done | bytes 786464 | tf_op jit(solution)/shard_map/ppermute | solution.py:14
  1253.2 353.0 %conditional.10 = (bf16[256,1536]{1,0:T(8,128)(2,1)}, f32[1536,48]{0,1:T(8,128)}, f32[4,3328]{1,0:T(4,128)}, f32[3328]{0:T(1024)}, f32[48]{0:T(128)}, /*index=5*...) conditional(s32[]{:T(128)} %convert_element_type.339, ...), branch_computations={%region_52.54_spmd, %region_53.84_spmd} | conditional | flops 20592838656 | bytes 781147136 | solution.py:255
  1286.9 60.2 %while.245 = (s32[]{:T(128)}, f32[48,64,128]{2,1,0:T(8,128)S(1)}, f32[2,128,48,64]{1,3,2,0:T(8,128)}, f32[2,48,128,128]{3,2,1,0:T(8,128)}, f32[2,128,128]{1,2,0:...) while((s32[]{:T(128)}, f32[48,64,128]{2,1,0:T(8,128)S(1)}, ...), condition=%wide.region_56.57_spmd.clone.clone, body=%wide.region_54.56_spmd.clone.clone.sunk | while | flops 1847734272 | bytes 84601144 | solution.py:57
  1393.8 68.0 %while.246 = (s32[]{:T(128)}, f32[48,64,128]{2,1,0:T(8,128)S(1)}, f32[2,128,48,64]{1,3,2,0:T(8,128)}, f32[2,128,48]{2,1,0:T(8,128)S(1)}, f32[2,128,128]{2,1,0:T(...) while((s32[]{:T(128)}, f32[48,64,128]{2,1,0:T(8,128)S(1)}, ...), condition=%wide.region_68.69_spmd.clone.clone, body=%wide.region_59.68_spmd.clone.clone.sunk | while | flops 3687632896 | bytes 91598432 | solution.py:57
  1493.6 17.5 convolution_bitcast_fusion.3
  1511.0 39.5 %copy.772 = f32[1536,6400]{1,0:T(8,128)} copy(f32[1536,6400]{0,1:T(8,128)} %convolution_bitcast_fusion.3) | data formatting | bytes 78643200 | tf_op jit(solution)/shard_map/cond | solution.py:255
  1587.4 18.8 copy.774
  1610.5 350.8 %conditional.11 = (f32[1536,48]{0,1:T(8,128)}, f32[4,3328]{1,0:T(4,128)}, f32[3328]{0:T(1024)}, f32[48]{0:T(128)}, f32[48]{0:T(128)}, /*index=5*/f32[48]{0:T(128...) conditional(s32[]{:T(128)} %convert_element_type.338, ...), branch_computations={%region_83.85_spmd, %region_84.115_spmd} | conditional | flops 20592838656 | bytes 793205952 | solution.py:255
  1644.2 60.5 %while.247 = (s32[]{:T(128)}, f32[48,64,128]{2,1,0:T(8,128)S(1)}, f32[2,128,48,64]{1,3,2,0:T(8,128)}, f32[2,48,128,128]{3,2,1,0:T(8,128)}, f32[2,128,128]{1,2,0:...) while((s32[]{:T(128)}, f32[48,64,128]{2,1,0:T(8,128)S(1)}, ...), condition=%wide.region_87.88_spmd.clone.clone, body=%wide.region_85.87_spmd.clone.clone.sunk | while | flops 1847734272 | bytes 84601144 | solution.py:57
  1751.6 68.0 %while.248 = (s32[]{:T(128)}, f32[48,64,128]{2,1,0:T(8,128)S(1)}, f32[2,128,48,64]{1,3,2,0:T(8,128)}, f32[2,128,48]{2,1,0:T(8,128)S(1)}, f32[2,128,128]{2,1,0:T(...) while((s32[]{:T(128)}, f32[48,64,128]{2,1,0:T(8,128)S(1)}, ...), condition=%wide.region_99.100_spmd.clone.clone, body=%wide.region_90.99_spmd.clone.clone.sunk | while | flops 3687632896 | bytes 91598432 | solution.py:57
  1851.1 17.4 convolution_bitcast_fusion.6
  1868.5 39.5 %copy.776 = f32[1536,6400]{1,0:T(8,128)} copy(f32[1536,6400]{0,1:T(8,128)} %convolution_bitcast_fusion.6) | data formatting | bytes 78643200 | tf_op jit(solution)/shard_map/cond | solution.py:255
  1942.5 18.6 copy.778
  1961.3 22.4 add_convert_fusion.10
  1983.8 44.0 %add_convert_fusion.9 = bf16[1536,6400]{1,0:T(8,128)(2,1)} fusion(f32[1536,6400]{1,0:T(8,128)} %get-tuple-element.5079, f32[1536,6400]{1,0:T(8,128)} %get-tuple-element.5075, f32[1536,6400]{1,0:T(8,128)} %get-tuple-element.5077), kind=kLoop, calls=%fused_computation.929 | loop fusion | flops 29491200 | bytes 137625600 | tf_op jit(solution)/shard_map/convert_element_type | solution.py:266
  2032.3 111.4 %reduce-scatter.11.cloned.1.call-done = bf16[768,1536]{1,0:T(8,128)(2,1)} async-done(((bf16[3072,1536]{1,0:T(8,128)(2,1)}), bf16[768,1536]{1,0:T(8,128)(2,1)}) %reduce-scatter.11.cloned.1.call-update) | async-done | bytes 2359312 | tf_op jit(solution)/shard_map/reduce_scatter | solution.py:271
  2143.6 329.7 %reduce-scatter.9.cloned.1.call-done = bf16[384,6400]{1,0:T(8,128)(2,1)} async-done(((bf16[1536,6400]{1,0:T(8,128)(2,1)}), bf16[384,6400]{1,0:T(8,128)(2,1)}) %reduce-scatter.9.cloned.1.call-update) | async-done | bytes 4915216 | tf_op jit(solution)/shard_map/reduce_scatter | solution.py:265
  2484.8 19.4 all-reduce.63
  2507.4 16.6 reduce-scatter.13.cloned.1.call-done
  2525.0 18.1 all-reduce.61
  2547.7 133.1 %all-reduce.67.cloned.1.call-done = (bf16[1,384,6400]{2,1,0:T(8,128)(2,1)}, bf16[1,768,1536]{2,1,0:T(8,128)(2,1)}) async-done(((bf16[1,384,6400]{2,1,0:T(8,128)(2,1)}, bf16[1,768,1536]{2,1,0:T(8,128)(2,1)}), (bf16[1,384,6400]{2,1,0:T(8,128)(2,1)}, bf16[1,768,1536]{2,1,0:T(8,128)(2,1)})) %all-reduce.67.cloned.1.call-update) | async-done | bytes 7274512 | tf_op jit(solution)/shard_map/psum | solution.py:296
  (1131 shorter events, 909.8 us)
Async XLA Ops:
  7.2 199.3 %all-gather.5.cloned.1.call-start = ((), (), s32[]{:S(2)}) async-start(), calls=%async_computation.4 | async-start | bytes 11796480 | tf_op jit(solution)/shard_map/all_gather | solution.py:174
  7.9 535.0 %all-gather.9.cloned.1.call-start = ((), (), s32[]{:S(2)}) async-start(), calls=%async_computation.8 | async-start | bytes 24576000 | tf_op jit(solution)/shard_map/all_gather | solution.py:172
  8.7 870.0 %all-gather.7.cloned.1.call-start = ((), (), s32[]{:S(2)}) async-start(), calls=%async_computation.5 | async-start | bytes 24576000 | tf_op jit(solution)/shard_map/all_gather | solution.py:223
  9.4 62.7 %copy-start.252 = (bf16[1,384,48]{1,2,0:T(8,128)(2,1)S(1)}, bf16[1,384,48]{1,2,0:T(8,128)(2,1)}, u32[]{:S(2)}) copy-start(bf16[1,384,48]{1,2,0:T(8,128)(2,1)} %param.46) | copy-start | bytes 110596
  9.4 62.8 %copy-start.276 = (bf16[1,832]{1,0:T(2,128)(2,1)S(1)}, bf16[1,832]{1,0:T(2,128)(2,1)}, u32[]{:S(2)}) copy-start(bf16[1,832]{1,0:T(2,128)(2,1)} %param.49) | copy-start | bytes 4996
  9.4 62.8 %copy-start.277 = (bf16[1,768]{1,0:T(2,128)(2,1)S(1)}, bf16[1,768]{1,0:T(2,128)(2,1)}, u32[]{:S(2)}) copy-start(bf16[1,768]{1,0:T(2,128)(2,1)} %param.54) | copy-start | bytes 4612
  9.5 81.0 %copy-start.291 = (bf16[1,384]{1,0:T(2,128)(2,1)S(1)}, bf16[1,384]{1,0:T(2,128)(2,1)}, u32[]{:S(2)}) copy-start(bf16[1,384]{1,0:T(2,128)(2,1)} %param.53) | copy-start | bytes 2308
  9.5 95.2 %copy-start.292 = (bf16[1,12]{1,0:T(2,128)(2,1)S(1)}, bf16[1,12]{1,0:T(2,128)(2,1)}, u32[]{:S(2)}) copy-start(bf16[1,12]{1,0:T(2,128)(2,1)} %param.51) | copy-start | bytes 76
  9.5 95.5 %copy-start.293 = (bf16[1,12]{1,0:T(2,128)(2,1)S(1)}, bf16[1,12]{1,0:T(2,128)(2,1)}, u32[]{:S(2)}) copy-start(bf16[1,12]{1,0:T(2,128)(2,1)} %param.52) | copy-start | bytes 76
  9.5 95.7 %copy-start.294 = (bf16[1,12]{1,0:T(2,128)(2,1)S(1)}, bf16[1,12]{1,0:T(2,128)(2,1)}, u32[]{:S(2)}) copy-start(bf16[1,12]{1,0:T(2,128)(2,1)} %param.50) | copy-start | bytes 76
  9.5 96.1 %copy-start.275 = (s32[2,1]{0,1:T(1,128)S(1)}, s32[2,1]{0,1:T(1,128)}, u32[]{:S(2)}) copy-start(s32[2,1]{0,1:T(1,128)} %param.44) | copy-start | bytes 28
  9.5 136.0 %copy-start.94 = (bf16[1,2,1,256,1536]{4,3,2,1,0:T(8,128)(2,1)S(1)}, bf16[1,2,1,256,1536]{4,3,2,1,0:T(8,128)(2,1)}, u32[]{:S(2)}) copy-start(bf16[1,2,1,256,1536]{4,3,2,1,0:T(8,128)(2,1)} %param.43) | copy-start | bytes 4718596
  9.5 2134.1 %reduce-scatter.11.cloned.1.call-start = ((), (), s32[]{:S(2)}) async-start(), calls=%async_computation.7 | async-start | bytes 11796480 | tf_op jit(solution)/shard_map/reduce_scatter | solution.py:271
  72.1 470.8 %copy-start.117 = (bf16[1,4,3328]{2,1,0:T(4,128)(2,1)}, bf16[1,4,3328]{2,1,0:T(4,128)(2,1)S(1)}, u32[]{:S(2)}) copy-start(bf16[1,4,3328]{2,1,0:T(4,128)(2,1)S(1)} %copy.734) | copy-start | bytes 79876
  90.5 789.2 %copy-start.178 = (bf16[3072]{0:T(1024)(128)(2,1)}, bf16[3072]{0:T(1024)(128)(2,1)S(1)}, u32[]{:S(2)}) copy-start(bf16[3072]{0:T(1024)(128)(2,1)S(1)} %reduce.32) | copy-start | bytes 18436
  104.6 438.3 %copy-start.192 = (bf16[1536]{0:T(1024)(128)(2,1)}, bf16[1536]{0:T(1024)(128)(2,1)S(1)}, u32[]{:S(2)}) copy-start(bf16[1536]{0:T(1024)(128)(2,1)S(1)} %reduce.31) | copy-start | bytes 9220
  119.5 423.4 %copy-start.295 = (bf16[48]{0:T(256)(128)(2,1)}, bf16[48]{0:T(256)(128)(2,1)S(1)}, u32[]{:S(2)}) copy-start(bf16[48]{0:T(256)(128)(2,1)S(1)} %get-tuple-element.5482) | copy-start | bytes 292
  119.5 423.4 %copy-start.301 = (bf16[48]{0:T(256)(128)(2,1)}, bf16[48]{0:T(256)(128)(2,1)S(1)}, u32[]{:S(2)}) copy-start(bf16[48]{0:T(256)(128)(2,1)S(1)} %get-tuple-element.5483) | copy-start | bytes 292
  119.5 760.2 %copy-start.183 = (bf16[3328]{0:T(1024)(128)(2,1)}, bf16[3328]{0:T(1024)(128)(2,1)S(1)}, u32[]{:S(2)}) copy-start(bf16[3328]{0:T(1024)(128)(2,1)S(1)} %get-tuple-element.5481) | copy-start | bytes 19972
  146.5 396.5 %copy-start.51 = (bf16[256,1536]{1,0:T(8,128)(2,1)}, bf16[256,1536]{1,0:T(8,128)(2,1)S(1)}, u32[]{:S(2)}) copy-start(bf16[256,1536]{1,0:T(8,128)(2,1)S(1)} %get-tuple-element.5529) | copy-start | bytes 2359300
  656.7 3.4 collective-permute-start
  776.8 4.6 collective-permute-start.1
  912.6 340.6 %collective-permute-start.2 = (bf16[256,1536]{1,0:T(8,128)(2,1)}, bf16[256,1536]{1,0:T(8,128)(2,1)S(1)}, u32[]{:S(2)}, u32[]{:S(2)}) collective-permute-start(bf16[256,1536]{1,0:T(8,128)(2,1)} %get-tuple-element.2930), channel_id=1, source_target_pairs={{16,0},{17,1},{18,2},{19,3},{20,4},{21,5},{22,6},{23,7},{24,8},{25... | collective-permute-start | bytes 2359304 | tf_op jit(solution)/shard_map/ppermute | solution.py:14
  1511.0 39.5 %copy-start.151 = (f32[2,128,48]{2,1,0:T(8,128)S(1)}, f32[2,128,48]{2,1,0:T(8,128)}, u32[]{:S(2)}) copy-start(f32[2,128,48]{2,1,0:T(8,128)} %copy-done.150) | copy-start | bytes 147460 | tf_op jit(solution)/shard_map/cond
  1511.0 40.2 %copy-start.43 = (f32[256,3072]{0,1:T(8,128)S(1)}, f32[256,3072]{0,1:T(8,128)}, u32[]{:S(2)}) copy-start(f32[256,3072]{0,1:T(8,128)} %copy.686) | copy-start | bytes 9437188 | tf_op jit(solution)/shard_map/cond
  1606.2 4.4 collective-permute-start.3
  1868.5 40.2 %copy-start.44 = (f32[256,3072]{0,1:T(8,128)S(1)}, f32[256,3072]{0,1:T(8,128)}, u32[]{:S(2)}) copy-start(f32[256,3072]{0,1:T(8,128)} %copy.715) | copy-start | bytes 9437188 | tf_op jit(solution)/shard_map/cond
  1983.7 489.6 %reduce-scatter.9.cloned.1.call-start = ((), (), s32[]{:S(2)}) async-start(), calls=%async_computation.6 | async-start | bytes 24576000 | tf_op jit(solution)/shard_map/reduce_scatter | solution.py:265
  2027.8 478.3 %reduce-scatter.15.cloned.1.call-start = ((), (), s32[]{:S(2)}) async-start(), calls=%async_computation.10 | async-start | bytes 1064960
  2030.0 494.0 %reduce-scatter.13.cloned.1.call-start = ((), (), s32[]{:S(2)}) async-start(), calls=%async_computation.9 | async-start | bytes 491520
  2032.2 648.6 %all-reduce.67.cloned.1.call-start = ((), (), s32[]{:S(2)}) async-start(), calls=%async_computation.11 | async-start | bytes 14548992 | tf_op jit(solution)/shard_map/psum | solution.py:296
  2506.1 181.8 %copy-start.115 = (bf16[1,2,1,256,1536]{4,3,2,1,0:T(8,128)(2,1)}, bf16[1,2,1,256,1536]{4,3,2,1,0:T(8,128)(2,1)S(1)}, u32[]{:S(2)}) copy-start(bf16[1,2,1,256,1536]{4,3,2,1,0:T(8,128)(2,1)S(1)} %bitcast_dynamic-update-slice_fusion.28) | copy-start | bytes 4718596
  (262 other events, 1024.7 us)
Sparse Core Ops, SparseCore 0:
  9.6 196.9 all-gather.4
  208.1 334.8 all-gather.8
  544.5 334.1 all-gather.6
  1983.8 159.7 reduce-scatter.10
  2145.9 327.4 reduce-scatter.8
  2476.1 26.1 reduce-scatter.14
  2504.5 19.4 reduce-scatter.12
  2527.7 153.0 all-reduce.66
